TPU v7x, 32 devices: a whole 2x2x4 slice. The times are simulated.
32 devices in a mesh: grp: 4 (over z), loc: 8 (over y, x, core).
Axes of the slice: x: 2, y: 2, z: 4, core: 2. Of those that a mesh axis runs over, the one named last changes fastest.
Arguments:
- tokens: bfloat16 [4096, 2048], P(('grp', 'loc')), may hold values from -6 to 6
- expert_ids: int32 [4096, 6], P(('grp', 'loc')), may hold values from 0 to 15, as said below
- gate_weights: bfloat16 [4096, 6], P(('grp', 'loc')), may hold values from 0.099609375 to 1
- w_gate: bfloat16 [32, 2048, 704], P(('grp', 'loc')), may hold values from -0.125 to 0.125
- w_up: bfloat16 [32, 2048, 704], P(('grp', 'loc')), may hold values from -0.125 to 0.125
- w_down: bfloat16 [32, 704, 2048], P(('grp', 'loc')), may hold values from -0.15625 to 0.15625
Outputs:
- moe_out: bfloat16 [4096, 2048], P(('grp', 'loc'))
Inputs may be any that keep to these rules, and one draw needn't show every extreme that they name: `expert_ids`: each row names 6 different experts in increasing order; they lie in exactly 4 of the 4 groups, expert e belonging to group e // 4.
All inputs are finite; a program needn't handle non-finite values.
Results may differ from a plain program's by a relative error of at most 0.008.
Values may be sent and summed in bfloat16 or wider, within the bound.
A program may use at most 128 MiB of HBM per device.

v0:
```python
import jax
import jax.numpy as jnp
from jax import lax
from jax.sharding import PartitionSpec as P


def silu_ffn(row_block, w_gate, w_up, w_down):
    row_shape = row_block.shape
    flat_rows = row_block.reshape(-1, row_shape[-1])
    gate_proj = jnp.dot(flat_rows, w_gate[0], preferred_element_type=jnp.float32)
    up_proj = jnp.dot(flat_rows, w_up[0], preferred_element_type=jnp.float32)
    hidden = (jax.nn.silu(gate_proj) * up_proj).astype(jnp.bfloat16)
    return (
        jnp.dot(hidden, w_down[0], preferred_element_type=jnp.float32)
        .astype(jnp.bfloat16)
        .reshape(row_shape)
    )


def with_zero_row(table):
    return jnp.concatenate([table, jnp.zeros((1, table.shape[1]), table.dtype)], axis=0)


def per_device(tokens, expert_ids, gate_weights, w_gate, w_up, w_down):
    groups = lax.axis_size("grp")
    loc_count = lax.axis_size("loc")
    experts = groups * loc_count // 2
    per_group = loc_count // 2
    tok_count, top_count = expert_ids.shape
    model_width = tokens.shape[1]
    capacity = 3 * tok_count * top_count // (2 * experts)
    flat_ids = expert_ids.reshape(-1)
    onehot = (flat_ids[:, None] == jnp.arange(experts, dtype=jnp.int32)[None, :]).astype(jnp.int32)
    slot_of = jnp.sum((jnp.cumsum(onehot, axis=0) - onehot) * onehot, axis=1).reshape(
        tok_count, top_count
    )
    is_kept = slot_of < capacity
    home_group = expert_ids // per_group
    token_index = jnp.arange(tok_count, dtype=jnp.int32)
    group_range = jnp.arange(groups, dtype=jnp.int32)
    padded = with_zero_row(tokens)
    place_at = jnp.where(is_kept, expert_ids * capacity + slot_of, experts * capacity)
    source_of = (
        jnp.full((experts * capacity + 1,), tok_count, jnp.int32)
        .at[place_at.reshape(-1)]
        .set(jnp.repeat(token_index, top_count))[:-1]
    )
    outgoing = padded[source_of].reshape(experts, 1, capacity, model_width)
    outgoing = jnp.broadcast_to(outgoing, (experts, 2, capacity, model_width)).reshape(
        2 * experts, capacity, model_width
    )
    returned = lax.all_to_all(
        silu_ffn(
            lax.all_to_all(outgoing, ("grp", "loc"), split_axis=0, concat_axis=0, tiled=True),
            w_gate,
            w_up,
            w_down,
        ),
        ("grp", "loc"),
        split_axis=0,
        concat_axis=0,
        tiled=True,
    )
    halves = returned.reshape(experts, 2, capacity, model_width)
    first_half = with_zero_row(halves[:, 0].reshape(-1, model_width))[place_at]
    second_half = with_zero_row(halves[:, 1].reshape(-1, model_width))[place_at]
    weights = jnp.where(is_kept, gate_weights.astype(jnp.float32), jnp.float32(0.0))
    combined = weights[:, :, None] * (
        first_half.astype(jnp.float32) + second_half.astype(jnp.float32)
    )
    group_mask = (home_group[:, :, None] == group_range[None, None, :]).astype(jnp.float32)
    group_sum = jnp.einsum("tkg,tkd->tgd", group_mask, combined, precision=lax.Precision.HIGHEST)
    group_part = lax.optimization_barrier(group_sum.astype(jnp.bfloat16))
    return jnp.sum(group_part.astype(jnp.float32), axis=1).astype(jnp.bfloat16)


def solution(mesh):
    in_specs = (
        P(("grp", "loc"), None),
        P(("grp", "loc"), None),
        P(("grp", "loc"), None),
        P(("grp", "loc"), None, None),
        P(("grp", "loc"), None, None),
        P(("grp", "loc"), None, None),
    )
    out_specs = P(("grp", "loc"), None)
    return jax.shard_map(
        per_device, mesh=mesh, in_specs=in_specs, out_specs=out_specs, check_vma=False
    )
```

profile of v0, /device:TPU:0, one launch (start us, length us, event | category | flops | bytes accessed | tf_op | source)
XLA Modules:
  0.0 551.7 jit_solution(5272143804177138845)
XLA Ops:
  0.0 0.0 copy-start
  0.0 0.8 broadcast_multiply_fusion
  0.8 0.8 copy.11
  1.7 0.1 eq.45
  1.8 0.1 eq.41
  2.0 0.1 copy.20
  2.1 1.7 reduce-window.6
  3.8 0.3 slice_reduce_fusion
  4.1 0.1 fusion.17
  4.2 0.1 reshape.71
  4.3 0.0 copy-start.3
  4.3 0.7 compare_select_fusion
  5.0 0.1 reshape.72
  5.2 0.1 reshape.106
  5.3 3.4 scatter_custom_fusion
  8.7 0.0 copy-done.3
  8.7 1.1 concatenate.9
  9.8 5.9 %gather_fusion = bf16[1152,2048]{1,0:T(8,128)(2,1)} fusion(bf16[129,2048]{1,0:T(8,128)(2,1)S(1)} %concatenate.9, s32[2048]{0:T(1024)S(1)} %pad_clamp_fusion), kind=kCustom, calls=%fused_computation | custom fusion | bytes 9441792 | tf_op jit(solution)/shard_map/gather | solution.py:48
  15.7 7.5 %broadcast_in_dim.39 = bf16[16,2,72,2048]{3,2,1,0:T(8,128)(2,1)} broadcast(bf16[16,72,2048]{2,1,0:T(8,128)(2,1)} %bitcast.45), dimensions={0,2,3} | broadcast | bytes 14155776 | tf_op jit(solution)/shard_map/broadcast_in_dim | solution.py:49
  23.2 0.0 copy-start.7
  23.2 213.3 %all_to_all.10 = bf16[32,72,2048]{2,1,0:T(8,128)(2,1)S(1)} all-to-all(bf16[32,72,2048]{2,1,0:T(8,128)(2,1)} %bitcast.44), channel_id=1, replica_groups=mesh['grp'=4,'loc'=8] {'grp','loc'}, dimensions={0} | all-to-all | bytes 18874368 | tf_op jit(solution)/shard_map/all_to_all | solution.py:54
  236.5 0.0 copy-start.2
  236.5 3.7 copy-done.2
  240.2 0.0 copy-done.7
  240.2 8.8 %fusion.10 = f32[2304,704]{0,1:T(8,128)} fusion(bf16[2304,2048]{1,0:T(8,128)(2,1)S(1)} %bitcast.49, bf16[1,2048,704]{1,2,0:T(8,128)(2,1)S(1)} %copy-done.7), kind=kOutput, calls=%fused_computation.14 | convolution fusion | flops 6643777536 | bytes 18808832 | tf_op jit(solution)/shard_map/dot_general | solution.py:10
  249.0 0.0 copy-done
  249.0 24.7 %convolution_convert_fusion = bf16[2304,2048]{1,0:T(8,128)(2,1)} fusion(f32[2304,704]{0,1:T(8,128)} %fusion.10, bf16[2304,2048]{1,0:T(8,128)(2,1)} %bitcast.50, bf16[1,704,2048]{2,1,0:T(8,128)(2,1)S(1)} %copy-done, bf16[1,2048,704]{1,2,0:T(8,128)(2,1)} %param.10), kind=kOutput, calls=%fused_computation.4 | convolution fusion | flops 13302005760 | bytes 31129600 | tf_op jit(solution)/shard_map/dot_general | solution.py:14
  273.7 0.0 copy-start.6
  273.7 0.0 copy-start.5
  273.7 0.0 copy-start.4
  273.7 4.1 all-to-all-start.1
  277.8 0.0 copy-done.6
  277.9 0.1 copy.18
  278.0 0.0 copy-done.5
  278.0 0.1 reshape.88
  278.2 0.0 copy-done.4
  278.2 208.5 %all-to-all-done.1 = bf16[32,72,2048]{2,1,0:T(8,128)(2,1)} async-done(((bf16[32,72,2048]{2,1,0:T(8,128)(2,1)}), bf16[32,72,2048]{2,1,0:T(8,128)(2,1)}, u32[]{:S(2)}, u32[]{:S(2)}) %all-to-all-start.1) | async-done | bytes 9437216 | tf_op jit(solution)/shard_map/all_to_all | solution.py:52
  486.7 7.5 %fusion.23 = (bf16[16,1,72,2048]{3,2,1,0:T(8,128)(2,1)S(1)}, bf16[16,1,72,2048]{3,2,1,0:T(8,128)(2,1)}) fusion(bf16[16,2,72,2048]{3,2,1,0:T(8,128)(2,1)} %bitcast.8), kind=kLoop, calls=%fused_computation.47 | loop fusion | bytes 18874368 | tf_op jit(solution)/shard_map/slice | solution.py:65
  494.2 5.2 concatenate.11
  499.4 2.8 concatenate.10
  502.1 10.1 %gather_fusion.2 = bf16[768,2048]{1,0:T(8,128)(2,1)} fusion(bf16[1153,2048]{1,0:T(8,128)(2,1)} %concatenate.11, s32[1024]{0:T(1024)S(1)} %pad_clamp_fusion.1), kind=kCustom, calls=%fused_computation.2 | custom fusion | bytes 6294528 | tf_op jit(solution)/shard_map/gather | solution.py:66
  512.2 10.1 %gather_fusion.1 = bf16[768,2048]{1,0:T(8,128)(2,1)} fusion(bf16[1153,2048]{1,0:T(8,128)(2,1)} %concatenate.10, s32[1024]{0:T(1024)S(1)} %pad_clamp_fusion.1), kind=kCustom, calls=%fused_computation.1 | custom fusion | bytes 6294528 | tf_op jit(solution)/shard_map/gather | solution.py:65
  522.3 6.9 %convert_add_fusion = f32[768,2048]{1,0:T(8,128)} fusion(bf16[768,2048]{1,0:T(8,128)(2,1)} %gather_fusion.2, bf16[768,2048]{1,0:T(8,128)(2,1)} %gather_fusion.1), kind=kLoop, calls=%fused_computation.8 | loop fusion | flops 4718592 | bytes 12582912 | tf_op jit(solution)/shard_map/add | solution.py:69
  529.2 0.0 copy-start.1
  529.2 8.0 %reshape.117 = f32[128,6,2048]{2,1,0:T(8,128)} reshape(f32[768,2048]{1,0:T(8,128)} %convert_add_fusion) | data formatting | bytes 12582912 | tf_op jit(solution)/shard_map/add | solution.py:69
  537.2 9.6 %fusion.4 = bf16[128,4,2048]{2,1,0:T(4,128)(2,1)} fusion(f32[128,6,2048]{2,1,0:T(8,128)} %reshape.117, f32[128,6]{1,0:T(8,128)S(1)} %broadcast_select_fusion, s32[128,6]{1,0:T(8,128)S(1)} %add_select_fusion), kind=kOutput, calls=%fused_computation.11 | convolution fusion | flops 78121984 | bytes 8394752 | tf_op jit(solution)/shard_map/tkg,tkd->tgd/dot_general | solution.py:72
  546.7 5.0 reduce_sum.22
  551.7 0.0 copy-done.1
  (9 shorter events, 0.1 us)
Async XLA Ops:
  0.0 249.0 %copy-start = (bf16[1,704,2048]{2,1,0:T(8,128)(2,1)S(1)}, bf16[1,704,2048]{2,1,0:T(8,128)(2,1)}, u32[]{:S(2)}) copy-start(bf16[1,704,2048]{2,1,0:T(8,128)(2,1)} %param.11) | copy-start | bytes 8650756
  4.3 4.4 copy-start.3
  23.2 217.0 %copy-start.7 = (bf16[1,2048,704]{1,2,0:T(8,128)(2,1)S(1)}, bf16[1,2048,704]{1,2,0:T(8,128)(2,1)}, u32[]{:S(2)}) copy-start(bf16[1,2048,704]{1,2,0:T(8,128)(2,1)} %param.9) | copy-start | bytes 8650756
  236.5 3.7 copy-start.2
  273.7 4.1 copy-start.6
  273.7 4.2 copy-start.5
  273.7 4.4 copy-start.4
  273.7 212.9 %all-to-all-start.1 = ((bf16[32,72,2048]{2,1,0:T(8,128)(2,1)}), bf16[32,72,2048]{2,1,0:T(8,128)(2,1)}, u32[]{:S(2)}, u32[]{:S(2)}) async-start(bf16[32,72,2048]{2,1,0:T(8,128)(2,1)} %bitcast.48), calls=%async_computation.1 | async-start | bytes 18874368 | tf_op jit(solution)/shard_map/all_to_all | solution.py:52
  529.2 22.5 %copy-start.1 = (bf16[1,704,2048]{2,1,0:T(8,128)(2,1)S(1)}, bf16[1,704,2048]{2,1,0:T(8,128)(2,1)}, u32[]{:S(2)}) copy-start(bf16[1,704,2048]{2,1,0:T(8,128)(2,1)} %param.11) | copy-start | bytes 8650756
where the time goes:
time: 552 us
  blocking collectives  213 us (39%)
  waiting for transfers between devices  208 us (38%)
  local copies, waits for them, and re-layouts  67.3 us (12%)
  matrix products  43.1 us (8%)
  other arithmetic  15.3 us (3%)
    all_to_all x1, blocking collectives, per_device(): lax.all_to_all(outgoing, ('grp', 'loc'), split_axis=0, concat_axis=0, til...  213 us
    all_to_all x1, waiting for transfers between devices, per_device(): lax.all_to_all(silu_ffn(lax.all_to_all(outgoing, ('grp', 'loc'), split_ax...  208 us
    dot_general x1, matrix products, silu_ffn(): jnp.dot(hidden, w_down[0], preferred_element_type=jnp.float32)  24.7 us
  transfers between devices with their start and end apart: 1, of which 1 were waited for; matrix products, arithmetic and copies ran while one was open for 0% of the time, Pallas kernels for 0%

commit v1 on v0

--- a/solution.py
+++ b/solution.py
@@ -1,6 +1,9 @@
+import functools
 import jax
 import jax.numpy as jnp
 from jax import lax
+from jax.experimental import pallas as pl
+from jax.experimental.pallas import tpu as pltpu
 from jax.sharding import PartitionSpec as P
 
 
@@ -21,7 +24,7 @@
     return jnp.concatenate([table, jnp.zeros((1, table.shape[1]), table.dtype)], axis=0)
 
 
-def per_device(tokens, expert_ids, gate_weights, w_gate, w_up, w_down):
+def per_device_slots(tokens, expert_ids, gate_weights, w_gate, w_up, w_down):
     groups = lax.axis_size("grp")
     loc_count = lax.axis_size("loc")
     experts = groups * loc_count // 2
@@ -74,16 +77,285 @@
     return jnp.sum(group_part.astype(jnp.float32), axis=1).astype(jnp.bfloat16)
 
 
+MESH = pl.DeviceIdType.MESH
+F32 = jnp.float32
+BF16 = jnp.bfloat16
+
+
+def flip(index, bits):
+    out, step = index, 1
+    while step <= bits:
+        if bits & step:
+            out = out + step - 2 * step * (lax.rem(index // step, 2))
+        step *= 2
+    return out
+
+
+def moe_kernel(
+    groups, capacity, tok, info, gate_any, up_any, down_any, out,
+    w_gate, w_up, w_down, blocks, infos, rows, peer_out, hid, places, parts,
+    sum1, sum2, zsum, send_sem, recv_sem, load_sem,
+):
+    count, width = tok.shape
+    half = width // 2
+    padded = places.shape[2]
+    a_cols, b_cols = pl.ds(0, half), pl.ds(half, half)
+    grp, loc = lax.axis_index("grp"), lax.axis_index("loc")
+    expert = (grp * (2 * 4) + loc) // 2
+    partner = (grp, flip(loc, 1))
+
+    def peer(k, r):
+        return (flip(grp, k), flip(loc, 2 * r))
+
+    others = [(k, r) for k in range(groups) for r in range(4) if k or r]
+    barrier = pltpu.get_barrier_semaphore()
+    for k, r in others:
+        pl.semaphore_signal(barrier, inc=1, device_id=peer(k, r), device_id_type=MESH)
+    pl.semaphore_signal(barrier, inc=1, device_id=partner, device_id_type=MESH)
+
+    loads = [
+        pltpu.make_async_copy(src.at[0], dst, load_sem.at[i])
+        for i, (src, dst) in enumerate(((gate_any, w_gate), (up_any, w_up), (down_any, w_down)))
+    ]
+    for load in loads:
+        load.start()
+    pl.semaphore_wait(barrier, len(others) + 1)
+
+    copies = []
+
+    def send(src, dst, device):
+        i = len(copies)
+        copy = pltpu.make_async_remote_copy(
+            src_ref=src, dst_ref=dst, send_sem=send_sem.at[i], recv_sem=recv_sem.at[i],
+            device_id=device, device_id_type=MESH,
+        )
+        copy.start()
+        copies.append([copy, False])
+        return i
+
+    def got(i):
+        copies[i][0].wait_recv()
+
+    def sent(i):
+        if not copies[i][1]:
+            copies[i][0].wait_send()
+            copies[i][1] = True
+
+    info_copy = {kr: send(info, infos.at[kr[0], kr[1]], peer(*kr)) for kr in others}
+    z_copy = {}
+
+    def block(k, r):
+        return tok if k == 0 and r == 0 else blocks.at[k, r]
+
+    x_copy, y_copy, d_copy, row_copy, out_copy = {}, {}, {}, {}, {}
+    a1, b1, a2, b2, zs = {}, {}, {}, {}, {}
+
+    def spread(k):
+        if k:
+            got(z_copy[k])
+        src = block(k, 0)
+        x_copy[k, 0] = send(src.at[:, a_cols], blocks.at[k, 1, :, a_cols], peer(0, 1))
+        y_copy[k, 1] = send(src.at[:, b_cols], blocks.at[k, 2, :, b_cols], peer(0, 2))
+        x_copy[k, 1] = send(src.at[:, b_cols], blocks.at[k, 1, :, b_cols], peer(0, 1))
+        y_copy[k, 0] = send(src.at[:, a_cols], blocks.at[k, 2, :, a_cols], peer(0, 2))
+
+    def forward(k):
+        got(x_copy[k, 0])
+        d_copy[k, 0] = send(blocks.at[k, 1, :, a_cols], blocks.at[k, 3, :, a_cols], peer(0, 2))
+        got(y_copy[k, 1])
+        d_copy[k, 1] = send(blocks.at[k, 2, :, b_cols], blocks.at[k, 3, :, b_cols], peer(0, 1))
+
+    def pick(k):
+        row_at = lax.broadcasted_iota(jnp.int32, (count, count), 0)
+        col_at = lax.broadcasted_iota(jnp.int32, (count, count), 1)
+        earlier = jnp.where(row_at < col_at, 1.0, 0.0).astype(BF16)
+        slot_at = lax.broadcasted_iota(jnp.int32, (padded, count), 0).astype(F32)
+        for r in range(4):
+            if k or r:
+                got(info_copy[k, r])
+                table = infos[k, r]
+            else:
+                table = info[...]
+            match = table[:8] == expert.astype(F32)
+            used = jnp.sum(jnp.where(match, 1.0, 0.0), axis=0, keepdims=True)
+            weight = jnp.sum(jnp.where(match, table[8:], 0.0), axis=0, keepdims=True)
+            slot = jnp.dot(
+                jnp.broadcast_to(used, (16, count)).astype(BF16), earlier,
+                preferred_element_type=F32,
+            )[:1]
+            slot = jnp.where((used > 0.5) & (slot < capacity), slot, -1.0)
+            here = slot_at == jnp.broadcast_to(slot, (padded, count))
+            places[k, r] = jnp.where(
+                here, jnp.broadcast_to(weight, (padded, count)), 0.0
+            ).astype(BF16)
+            if r == 1:
+                got(x_copy[k, 1])
+            if r == 2:
+                got(y_copy[k, 0])
+            if r == 3:
+                got(d_copy[k, 0])
+                got(d_copy[k, 1])
+            chosen = jnp.where(here, 1.0, 0.0).astype(BF16)
+            rows[k, 0, r * padded : (r + 1) * padded, :] = jnp.dot(
+                chosen, block(k, r)[...], preferred_element_type=F32
+            ).astype(BF16)
+        row_copy[k] = send(rows.at[k, 0], rows.at[k, 1], partner)
+
+    def ffn(k, side):
+        if side == 0:
+            sent(row_copy[k])
+        else:
+            got(row_copy[k])
+        data = rows[k, side]
+        gate_proj = jnp.dot(data, w_gate[...], preferred_element_type=F32)
+        up_proj = jnp.dot(data, w_up[...], preferred_element_type=F32)
+        hid[...] = (gate_proj / (1.0 + jnp.exp(-gate_proj)) * up_proj).astype(BF16)
+        tile = width // 4
+
+        @pl.loop(0, 4)
+        def _(n):
+            cols = pl.ds(pl.multiple_of(n * tile, tile), tile)
+            rows[k, side, :, cols] = jnp.dot(
+                hid[...], w_down[:, cols], preferred_element_type=F32
+            ).astype(BF16)
+
+        if side == 1:
+            out_copy[k] = send(rows.at[k, 1], peer_out.at[k], partner)
+
+    def combine(k):
+        got(out_copy[k])
+        tile = width // 4
+        for r in range(4):
+            back = places[k, r]
+            span = pl.ds(r * padded, padded)
+
+            @pl.loop(0, 4)
+            def _(n):
+                cols = pl.ds(pl.multiple_of(n * tile, tile), tile)
+                total = lax.dot_general(
+                    back, rows[k, 0, span, cols], (((0,), (0,)), ((), ())),
+                    preferred_element_type=F32,
+                ) + lax.dot_general(
+                    back, peer_out[k, span, cols], (((0,), (0,)), ((), ())),
+                    preferred_element_type=F32,
+                )
+                parts[k, r, :, cols] = total.astype(BF16)
+
+        a1[k, 2] = send(parts.at[k, 3, :, a_cols], sum1.at[k, 1, :, a_cols], peer(0, 1))
+        b1[k, 1] = send(parts.at[k, 3, :, b_cols], sum1.at[k, 1, :, b_cols], peer(0, 2))
+        a1[k, 0] = send(parts.at[k, 1, :, a_cols], sum1.at[k, 0, :, a_cols], peer(0, 1))
+        b1[k, 0] = send(parts.at[k, 2, :, b_cols], sum1.at[k, 0, :, b_cols], peer(0, 2))
+
+    def add(k, r, cols, other):
+        parts[k, r, :, cols] = (
+            parts[k, r, :, cols].astype(F32) + other.astype(F32)
+        ).astype(BF16)
+
+    def reduce_one(k):
+        got(a1[k, 2])
+        add(k, 2, a_cols, sum1[k, 1, :, a_cols])
+        a2[k] = send(parts.at[k, 2, :, a_cols], sum2.at[k, :, a_cols], peer(0, 2))
+        got(b1[k, 1])
+        add(k, 1, b_cols, sum1[k, 1, :, b_cols])
+        b2[k] = send(parts.at[k, 1, :, b_cols], sum2.at[k, :, b_cols], peer(0, 1))
+
+    def reduce_two(k):
+        for first, second, cols in ((a1, a2, a_cols), (b1, b2, b_cols)):
+            got(first[k, 0])
+            got(second[k])
+            add(k, 0, cols, sum1[k, 0, :, cols].astype(F32) + sum2[k, :, cols].astype(F32))
+        if k:
+            zs[k] = send(parts.at[k, 0], zsum.at[k - 1], peer(k, 0))
+
+    spread(0)
+    for k in range(1, groups):
+        z_copy[k] = send(tok, blocks.at[k, 0], peer(k, 0))
+    spread(1)
+    forward(0)
+    for k in range(groups):
+        pick(k)
+        if k == 0:
+            for load in loads:
+                load.wait()
+        ffn(k, 0)
+        if k + 1 < groups:
+            forward(k + 1)
+        ffn(k, 1)
+        if k + 2 < groups:
+            spread(k + 2)
+        if k >= 1:
+            reduce_one(k - 1)
+        if k >= 2:
+            reduce_two(k - 2)
+        combine(k)
+    if groups >= 2:
+        reduce_two(groups - 2)
+    reduce_one(groups - 1)
+    reduce_two(groups - 1)
+    total = parts[0, 0].astype(F32)
+    for k in range(1, groups):
+        got(zs[k])
+        total = total + zsum[k - 1].astype(F32)
+    out[...] = total.astype(out.dtype)
+    for i in range(len(copies)):
+        sent(i)
+
+
+def per_device_direct(tokens, expert_ids, gate_weights, w_gate, w_up, w_down):
+    groups = lax.axis_size("grp")
+    experts = groups * lax.axis_size("loc") // 2
+    count, top_count = expert_ids.shape
+    width, units = w_gate.shape[1:]
+    capacity = 3 * count * top_count // (2 * experts)
+    padded = -(-capacity // 16) * 16
+    info = jnp.concatenate(
+        [
+            jnp.pad(expert_ids.T.astype(F32), ((0, 8 - top_count), (0, 0)), constant_values=-1.0),
+            jnp.pad(gate_weights.T.astype(F32), ((0, 8 - top_count), (0, 0))),
+        ],
+        axis=0,
+    )
+    copies = groups * 4 - 1 + groups - 1 + groups * 14 + groups - 1
+    vmem = pl.BlockSpec(memory_space=pltpu.VMEM)
+    hbm = pl.BlockSpec(memory_space=pl.ANY)
+    return pl.pallas_call(
+        functools.partial(moe_kernel, groups, capacity),
+        out_shape=jax.ShapeDtypeStruct((count, width), tokens.dtype),
+        in_specs=[vmem, vmem, hbm, hbm, hbm],
+        out_specs=vmem,
+        scratch_shapes=[
+            pltpu.VMEM((width, units), BF16),
+            pltpu.VMEM((width, units), BF16),
+            pltpu.VMEM((units, width), BF16),
+            pltpu.VMEM((groups, 4, count, width), BF16),
+            pltpu.VMEM((groups, 4, 16, count), F32),
+            pltpu.VMEM((groups, 2, 4 * padded, width), BF16),
+            pltpu.VMEM((groups, 4 * padded, width), BF16),
+            pltpu.VMEM((4 * padded, units), BF16),
+            pltpu.VMEM((groups, 4, padded, count), BF16),
+            pltpu.VMEM((groups, 4, count, width), BF16),
+            pltpu.VMEM((groups, 2, count, width), BF16),
+            pltpu.VMEM((groups, count, width), BF16),
+            pltpu.VMEM((groups - 1, count, width), BF16),
+            pltpu.SemaphoreType.DMA((copies,)),
+            pltpu.SemaphoreType.DMA((copies,)),
+            pltpu.SemaphoreType.DMA((3,)),
+        ],
+        compiler_params=pltpu.CompilerParams(
+            collective_id=0, has_side_effects=True, vmem_limit_bytes=67043328
+        ),
+    )(tokens, info, w_gate, w_up, w_down)
+
+
 def solution(mesh):
-    in_specs = (
-        P(("grp", "loc"), None),
-        P(("grp", "loc"), None),
-        P(("grp", "loc"), None),
-        P(("grp", "loc"), None, None),
-        P(("grp", "loc"), None, None),
-        P(("grp", "loc"), None, None),
-    )
-    out_specs = P(("grp", "loc"), None)
+    groups, locs = mesh.shape["grp"], mesh.shape["loc"]
+    direct = locs == 8 and groups in (2, 4)
+    spec = P(("grp", "loc"), None)
+    wide = P(("grp", "loc"), None, None)
     return jax.shard_map(
-        per_device, mesh=mesh, in_specs=in_specs, out_specs=out_specs, check_vma=False
-    )
+        per_device_direct if direct else per_device_slots,
+        mesh=mesh,
+        in_specs=(spec, spec, spec, wide, wide, wide),
+        out_specs=spec,
+        check_vma=False,
+    )

time: 552 us -> 195 us (0.35)
  blocking collectives: 213 us -> 0 us
  waiting for transfers between devices: 208 us -> 0 us
  Pallas kernels: 0 us -> 180 us
  local copies, waits for them, and re-layouts: 67.3 us -> 9.46 us
  matrix products: 43.1 us -> 0 us
  other arithmetic: 15.3 us -> 1.98 us
    all_to_all x1 -> x0, blocking collectives: 213 us -> none  [per_device(): lax.all_to_all(outgoing, ('grp', 'loc'), split_axis=0, concat_axis=0, til...]
    all_to_all x1 -> x0, waiting for transfers between devices: 208 us -> none  [per_device(): lax.all_to_all(silu_ffn(lax.all_to_all(outgoing, ('grp', 'loc'), split_ax...]
    pallas_call x0 -> x1, Pallas kernels: none -> 180 us  [per_device_direct(): pl.pallas_call(functools.partial(moe_kernel, groups, capacity), out_shape...]
    dot_general x3 -> x0, matrix products: 43.1 us -> none  [the longest x1 24.7 us: silu_ffn(): jnp.dot(hidden, w_down[0], preferred_element_type=jnp.float32)]
    gather x3 -> x0, local copies, waits for them, and re-layouts: 26 us -> none  [the longest x1 10.1 us: per_device(): second_half = with_zero_row(halves[:, 1].reshape(-1, model_width))[place_at]]
    concatenate x3 -> x0, local copies, waits for them, and re-layouts: 9.06 us -> none  [with_zero_row(): jnp.concatenate([table, jnp.zeros((1, table.shape[1]), table.dtype)], axi...]
    add x1 -> x0, local copies, waits for them, and re-layouts: 7.99 us -> none  [per_device(): first_half.astype(jnp.float32) + second_half.astype(jnp.float32)]
    slice x2 -> x0, local copies, waits for them, and re-layouts: 7.74 us -> none  [the longest x1 7.49 us: per_device(): first_half = with_zero_row(halves[:, 0].reshape(-1, model_width))[place_at]]
  transfers between devices with their start and end apart: 1 -> 0, of which waited for: 1 -> 0; matrix products, arithmetic and copies ran while one was open for 0% -> 0% of each run, Pallas kernels for 0% -> 0%
where the time goes in v1:
time: 195 us; the launch traced here: 191 us
  Pallas kernels  180 us (92%)
  local copies, waits for them, and re-layouts  9.46 us (5%)
  other arithmetic  1.98 us (1%)
    pallas_call x1, Pallas kernels, per_device_direct(): pl.pallas_call(functools.partial(moe_kernel, groups, capacity), out_shape...  180 us
    unnamed x5, local copies, waits for them, and re-layouts  9.46 us

profile of v1, /device:TPU:0, one launch (start us, length us, event | category | flops | bytes accessed | tf_op | source)
XLA Modules:
  0.0 191.1 jit_solution(4771015665749110759)
XLA Ops:
  0.0 0.7 convert_bitcast_fusion
  0.7 0.7 pad_convert_fusion
  1.4 0.6 select_maximum_fusion.info
  2.0 0.0 copy-start
  2.0 4.7 %copy.7.gate_any = bf16[1,2048,704]{2,1,0:T(8,128)(2,1)} copy(bf16[1,2048,704]{1,2,0:T(8,128)(2,1)} %param.9) | data formatting | bytes 5767168 | tf_op args[3]
  6.7 0.0 copy-done
  6.7 2.8 %copy.8.up_any = bf16[1,2048,704]{2,1,0:T(8,128)(2,1)} copy(bf16[1,2048,704]{1,2,0:T(8,128)(2,1)S(1)} %copy-done) | data formatting | bytes 5767168 | tf_op args[4]
  9.6 179.7 %shard_map.64 = bf16[128,2048]{1,0:T(8,128)(2,1)} custom-call(bf16[128,2048]{1,0:T(8,128)(2,1)} %tok.1, f32[16,128]{1,0:T(8,128)} %select_maximum_fusion.info, bf16[1,2048,704]{2,1,0:T(8,128)(2,1)} %copy.7.gate_any, bf16[1,2048,704]{2,1,0:T(8,128)(2,1)} %copy.8.up_any, bf16[1,704,2048]{2,1,0:T(8,128)(2,1)} %down_any.1), custom_call_target="tpu_custom_call" | custom-call | tf_op jit(solution)/shard_map/pallas_call | solution.py:321
  189.2 1.9 copy.10
Async XLA Ops:
  2.0 4.8 %copy-start = (bf16[1,2048,704]{1,2,0:T(8,128)(2,1)S(1)}, bf16[1,2048,704]{1,2,0:T(8,128)(2,1)}, u32[]{:S(2)}) copy-start(bf16[1,2048,704]{1,2,0:T(8,128)(2,1)} %param.10) | copy-start | bytes 8650756

commit v2 on v1

--- a/solution.py
+++ b/solution.py
@@ -225,7 +225,7 @@
     def combine(k):
         got(out_copy[k])
         tile = width // 4
-        for r in range(4):
+        for r in (3, 1, 2, 0):
             back = places[k, r]
             span = pl.ds(r * padded, padded)
 
@@ -241,10 +241,14 @@
                 )
                 parts[k, r, :, cols] = total.astype(BF16)
 
-        a1[k, 2] = send(parts.at[k, 3, :, a_cols], sum1.at[k, 1, :, a_cols], peer(0, 1))
-        b1[k, 1] = send(parts.at[k, 3, :, b_cols], sum1.at[k, 1, :, b_cols], peer(0, 2))
-        a1[k, 0] = send(parts.at[k, 1, :, a_cols], sum1.at[k, 0, :, a_cols], peer(0, 1))
-        b1[k, 0] = send(parts.at[k, 2, :, b_cols], sum1.at[k, 0, :, b_cols], peer(0, 2))
+            if r & 1:
+                a1[k, r - 1] = send(
+                    parts.at[k, r, :, a_cols], sum1.at[k, r // 2, :, a_cols], peer(0, 1)
+                )
+            if r & 2:
+                b1[k, r - 2] = send(
+                    parts.at[k, r, :, b_cols], sum1.at[k, r - 2, :, b_cols], peer(0, 2)
+                )
 
     def add(k, r, cols, other):
         parts[k, r, :, cols] = (
@@ -270,8 +274,8 @@
     spread(0)
     for k in range(1, groups):
         z_copy[k] = send(tok, blocks.at[k, 0], peer(k, 0))
+    forward(0)
     spread(1)
-    forward(0)
     for k in range(groups):
         pick(k)
         if k == 0:
@@ -280,18 +284,22 @@
         ffn(k, 0)
         if k + 1 < groups:
             forward(k + 1)
+        if k >= 3:
+            reduce_two(k - 2)
         ffn(k, 1)
         if k + 2 < groups:
             spread(k + 2)
+        if k >= 2:
+            reduce_one(k - 1)
         if k >= 1:
-            reduce_one(k - 1)
-        if k >= 2:
-            reduce_two(k - 2)
-        combine(k)
-    if groups >= 2:
+            combine(k)
+    combine(0)
+    if groups >= 3:
         reduce_two(groups - 2)
     reduce_one(groups - 1)
+    reduce_one(0)
     reduce_two(groups - 1)
+    reduce_two(0)
     total = parts[0, 0].astype(F32)
     for k in range(1, groups):
         got(zs[k])

time: 195 us -> 175 us (0.90)
  Pallas kernels: 180 us -> 161 us
    pallas_call x1, Pallas kernels: 180 us -> 161 us  [per_device_direct(): pl.pallas_call(functools.partial(moe_kernel, groups, capacity), out_shape...]
where the time goes in v2:
time: 175 us; the launch traced here: 172 us
  Pallas kernels  161 us (92%)
  local copies, waits for them, and re-layouts  9.46 us (5%)
  other arithmetic  1.98 us (1%)
    pallas_call x1, Pallas kernels, per_device_direct(): pl.pallas_call(functools.partial(moe_kernel, groups, capacity), out_shape...  161 us
    unnamed x5, local copies, waits for them, and re-layouts  9.46 us

profile of v2, /device:TPU:0, one launch (start us, length us, event | category | flops | bytes accessed | tf_op | source)
XLA Modules:
  0.0 172.2 jit_solution(9102866797320719731)
XLA Ops:
  0.0 0.7 convert_bitcast_fusion
  0.7 0.7 pad_convert_fusion
  1.4 0.6 select_maximum_fusion.info
  2.0 0.0 copy-start
  2.0 4.7 %copy.7.gate_any = bf16[1,2048,704]{2,1,0:T(8,128)(2,1)} copy(bf16[1,2048,704]{1,2,0:T(8,128)(2,1)} %param.9) | data formatting | bytes 5767168 | tf_op args[3]
  6.7 0.0 copy-done
  6.7 2.8 %copy.8.up_any = bf16[1,2048,704]{2,1,0:T(8,128)(2,1)} copy(bf16[1,2048,704]{1,2,0:T(8,128)(2,1)S(1)} %copy-done) | data formatting | bytes 5767168 | tf_op args[4]
  9.6 160.8 %shard_map.64 = bf16[128,2048]{1,0:T(8,128)(2,1)} custom-call(bf16[128,2048]{1,0:T(8,128)(2,1)} %tok.1, f32[16,128]{1,0:T(8,128)} %select_maximum_fusion.info, bf16[1,2048,704]{2,1,0:T(8,128)(2,1)} %copy.7.gate_any, bf16[1,2048,704]{2,1,0:T(8,128)(2,1)} %copy.8.up_any, bf16[1,704,2048]{2,1,0:T(8,128)(2,1)} %down_any.1), custom_call_target="tpu_custom_call" | custom-call | tf_op jit(solution)/shard_map/pallas_call | solution.py:329
  170.4 1.9 %copy.10 = bf16[128,2048]{1,0:T(8,128)(2,1)} copy(bf16[128,2048]{1,0:T(8,128)(2,1)} %shard_map.64) | data formatting | bytes 1048576
Async XLA Ops:
  2.0 4.8 %copy-start = (bf16[1,2048,704]{1,2,0:T(8,128)(2,1)S(1)}, bf16[1,2048,704]{1,2,0:T(8,128)(2,1)}, u32[]{:S(2)}) copy-start(bf16[1,2048,704]{1,2,0:T(8,128)(2,1)} %param.10) | copy-start | bytes 8650756
